TPU v7x, 32 devices: a whole 2x2x4 slice. The times are simulated.
32 devices in a mesh: seq: 8 (over z, x), head: 4 (over y, core).
Axes of the slice: x: 2, y: 2, z: 4, core: 2. Of those that a mesh axis runs over, the one named last changes fastest.
Arguments:
- queries: bfloat16 [4096, 4096], P('seq', 'head'), may hold values from -6 to 6
- keys: bfloat16 [4096, 4096], P('seq', 'head'), may hold values from -6 to 6
- values: bfloat16 [4096, 4096], P('seq', 'head'), may hold values from -6 to 6
- med_weight: float32 [2, 32, 4], P(None, 'head'), may hold values from -3 to 3
- coarse_weight: float32 [2, 32, 64], P(None, 'head'), may hold values from -0.75 to 0.75
- out_weight: bfloat16 [4096, 4096], P('head'), may hold values from -0.09375 to 0.09375
Outputs:
- mixed: bfloat16 [4096, 4096], P('seq', 'head')
All inputs are finite; a program needn't handle non-finite values.
Results may differ from a plain program's by a relative error of at most 0.013.
Values may be sent and summed in bfloat16 or wider, within the bound.
A program may use at most 128 MiB of HBM per device.

v0:
```python
import functools
import math

import jax
import jax.numpy as jnp
from jax import lax
from jax.experimental import pallas as pl
from jax.experimental.pallas import tpu as pltpu
from jax.sharding import PartitionSpec as P

HEAD_DIM = 128
MED = 4
COARSE = 64
CHUNKS = 2
MESH = pl.DeviceIdType.MESH
F32 = jnp.float32
BF16 = jnp.bfloat16


def mm(a, b):
    return jnp.dot(a, b, preferred_element_type=F32)


def mm_nt(a, b):
    return lax.dot_general(a, b, (((1,), (1,)), ((), ())), preferred_element_type=F32)


def split(w):
    hi = w.astype(BF16)
    return hi, (w - hi.astype(F32)).astype(BF16)


def kernel(
    n_seq, n_head, q_hbm, k_hbm, v_hbm, wm_ref, wc_ref, w_hbm, out_ref,
    q_v, k_v, v_v, w_v, vt, q_in, oe_out, le_out, oe_in, le_in,
    med_own, med_in, c_own, c_in, ck, cvt, o_loc, m_loc, l_loc, attn,
    pair_out, pair_in, far_out, far_in, acc,
    ld_sem, q_ss, q_rs, oe_ss, oe_rs, le_ss, le_rs, med_ss, med_rs, c_ss, c_rs,
    pair_ss, pair_rs, far_ss, far_rs,
):
    tok, feat = q_v.shape
    heads = feat // HEAD_DIM
    chunk = tok // CHUNKS
    n_med = tok // MED
    n_coarse = tok // COARSE
    width = out_ref.shape[1]
    scale = 1.0 / math.sqrt(HEAD_DIM)
    pos = lax.axis_index("seq")
    hd = lax.axis_index("head")
    groups = n_head // 2
    grp = hd // 2
    core = lax.rem(hd, 2)
    mate = grp * 2 + (1 - core)

    def remote(src, dst, ss, rs, **dev):
        return pltpu.make_async_remote_copy(
            src_ref=src, dst_ref=dst, send_sem=ss, recv_sem=rs,
            device_id=dev, device_id_type=MESH,
        )

    def hs(h):
        return pl.ds(pl.multiple_of(h * HEAD_DIM, HEAD_DIM), HEAD_DIM)

    loads = [
        pltpu.make_async_copy(s, d, ld_sem.at[n])
        for n, (s, d) in enumerate(((k_hbm, k_v), (v_hbm, v_v), (q_hbm, q_v), (w_hbm, w_v)))
    ]
    for ld in loads:
        ld.start()

    barrier = pltpu.get_barrier_semaphore()

    @pl.loop(1, n_seq)
    def _(d):
        pl.semaphore_signal(
            barrier, inc=1, device_id={"seq": lax.rem(pos + d, n_seq)}, device_id_type=MESH
        )

    @pl.loop(1, n_head)
    def _(d):
        pl.semaphore_signal(
            barrier, inc=1, device_id={"head": lax.rem(hd + d, n_head)}, device_id_type=MESH
        )

    @pl.loop(0, n_seq)
    def _(o):
        @pl.when(o >= pos)
        def _():
            c_in[o] = jnp.zeros(c_in.shape[1:], BF16)

    for slot in range(2):
        @pl.when(pos < 2 * slot + 2)
        def _():
            med_in[slot] = jnp.zeros(med_in.shape[1:], BF16)

    @pl.when(pos == 0)
    def _():
        oe_in[...] = jnp.zeros_like(oe_in)
        le_in[...] = jnp.full_like(le_in, -jnp.inf)

    pl.semaphore_wait(barrier, n_seq - 1 + n_head - 1)

    def q_copy(i):
        rows = pl.ds(i * chunk, chunk)
        return remote(
            q_hbm.at[rows], q_in.at[i], q_ss.at[i], q_rs.at[i], seq=jnp.maximum(pos - 1, 0)
        )

    def oe_copy(i, h):
        return remote(
            oe_out.at[i, h], oe_in.at[i, h], oe_ss.at[i, h], oe_rs.at[i, h],
            seq=jnp.minimum(pos + 1, n_seq - 1),
        )

    def le_copy(i):
        return remote(
            le_out.at[i], le_in.at[i], le_ss.at[i], le_rs.at[i],
            seq=jnp.minimum(pos + 1, n_seq - 1),
        )

    def med_copy(slot):
        src = med_own if slot == 0 else med_in.at[0]
        return remote(
            src, med_in.at[slot], med_ss.at[slot], med_rs.at[slot],
            seq=jnp.minimum(pos + 2, n_seq - 1),
        )

    def c_copy(to):
        return remote(c_own, c_in.at[pos], c_ss.at[to], c_rs.at[pos], seq=to)

    has_prev = pos >= 1
    has_next = pos < n_seq - 1

    @pl.when(has_prev)
    def _():
        for i in range(CHUNKS):
            q_copy(i).start()

    loads[0].wait()
    loads[1].wait()

    @pl.loop(0, heads)
    def _(h):
        kh = k_v[:, hs(h)]
        vh = v_v[:, hs(h)]
        vth = vh.T
        vt[h] = vth
        row = lax.broadcasted_iota(jnp.int32, (n_med, tok), 0)
        col = lax.broadcasted_iota(jnp.int32, (n_med, tok), 1)
        pick = (col // MED) == row
        hi, lo = split(jnp.where(pick, wm_ref[h], 0.0))
        med_own[0, h] = (mm(hi, kh) + mm(lo, kh)).astype(BF16)
        hi, lo = split(jnp.where(pick, wm_ref[heads + h], 0.0))
        med_own[1, h] = (mm_nt(vth, hi) + mm_nt(vth, lo)).astype(BF16)
        row = lax.broadcasted_iota(jnp.int32, (2 * n_coarse, tok), 0)
        col = lax.broadcasted_iota(jnp.int32, (2 * n_coarse, tok), 1) // COARSE
        hi, lo = split(jnp.where(col == row, wc_ref[h], 0.0))
        hi2, lo2 = split(jnp.where(col + n_coarse == row, wc_ref[heads + h], 0.0))
        c_own[h] = (mm(hi, kh) + mm(lo, kh) + mm(hi2, vh) + mm(lo2, vh)).astype(BF16)

    @pl.when(pos + 2 < n_seq)
    def _():
        med_copy(0).start()

    @pl.loop(0, n_seq)
    def _(to):
        @pl.when(to > pos)
        def _():
            c_copy(to).start()

    def edge(i):
        @pl.when(has_next)
        def _():
            q_copy(i).wait_recv()

            @pl.loop(0, heads)
            def _(h):
                q = q_in[i, :, hs(h)]
                s = mm_nt(k_v[:, hs(h)], q)
                s2 = jnp.where(pos >= 2, mm_nt(med_in[0, 0, h], q), -jnp.inf)
                m = jnp.maximum(
                    jnp.max(s, axis=0, keepdims=True), jnp.max(s2, axis=0, keepdims=True)
                )
                p = jnp.exp((s - m) * scale)
                p2 = jnp.exp((s2 - m) * scale)
                total = jnp.sum(p, axis=0, keepdims=True) + jnp.sum(p2, axis=0, keepdims=True)
                o = mm(vt[h], p.astype(BF16)) + mm(med_in[0, 1, h], p2.astype(BF16))
                oe_out[i, h] = (o / total).astype(BF16)
                le_out[i, h] = m * scale + jnp.log(total)
                oe_copy(i, h).start()

            le_copy(i).start()

    def local(i):
        keys = (i + 1) * chunk
        first = i * chunk

        @pl.loop(0, heads)
        def _(h):
            q = q_v[pl.ds(first, chunk), hs(h)]
            s = mm_nt(k_v[pl.ds(0, keys), hs(h)], q)
            key_at = lax.broadcasted_iota(jnp.int32, (keys, chunk), 0)
            query_at = lax.broadcasted_iota(jnp.int32, (keys, chunk), 1) + first
            parts = [(jnp.where(key_at <= query_at, s, -jnp.inf), vt[h, :, pl.ds(0, keys)])]
            for slot in range(2):
                s = mm_nt(med_in[slot, 0, h], q)
                parts.append((jnp.where(pos >= 2 * slot + 2, s, -jnp.inf), med_in[slot, 1, h]))
            s = mm_nt(ck[h], q)
            owner = lax.broadcasted_iota(jnp.int32, s.shape, 0) // n_coarse
            parts.append((jnp.where(owner < pos, s, -jnp.inf), cvt[h]))
            m = functools.reduce(
                jnp.maximum, [jnp.max(s, axis=0, keepdims=True) for s, _ in parts]
            )
            total = 0.0
            o = 0.0
            for s, vals in parts:
                p = jnp.exp((s - m) * scale)
                total = total + jnp.sum(p, axis=0, keepdims=True)
                o = o + mm(vals, p.astype(BF16))
            o_loc[i, h] = o
            m_loc[i, h] = m * scale
            l_loc[i, h] = total

    def combine(i):
        @pl.when(has_prev)
        def _():
            le_copy(i).wait_recv()

            @pl.loop(0, heads)
            def _(h):
                oe_copy(i, h).wait_recv()

        @pl.loop(0, heads)
        def _(h):
            lse = le_in[i, h]
            top = jnp.maximum(m_loc[i, h], lse)
            a = jnp.exp(m_loc[i, h] - top)
            e = jnp.exp(lse - top)
            inv = 1.0 / (l_loc[i, h] * a + e)
            o = o_loc[i, h] * (a * inv) + oe_in[i, h].astype(F32) * (e * inv)
            attn[i, :, hs(h)] = o.T.astype(BF16)

    tile = math.gcd(width, 512)

    def project(i, target, put):
        @pl.loop(0, width // tile)
        def _(j):
            cols = pl.ds(pl.multiple_of(target * width + j * tile, tile), tile)
            put(pl.ds(pl.multiple_of(j * tile, tile), tile), mm(attn[i], w_v[:, cols]))

    def pair_copy(i, o):
        return remote(
            pair_out.at[i, o], pair_in.at[i, o], pair_ss.at[i, o], pair_rs.at[i, o], head=mate
        )

    def far_copy(i, o):
        return remote(
            far_out.at[i, o - 1], far_in.at[i, o - 1], far_ss.at[i, o - 1], far_rs.at[i, o - 1],
            head=lax.rem(grp + o, groups) * 2 + core,
        )

    def mix(i):
        order = list(range(1, groups)) + [0]
        for o in order:
            there = lax.rem(grp + o, groups) * 2

            def put_pair(cols, value):
                pair_out[i, o, :, cols] = value.astype(BF16)

            project(i, there + (1 - core), put_pair)
            pair_copy(i, o).start()
            if o:
                def put_far(cols, value):
                    acc[i, :, cols] = value

                project(i, there + core, put_far)
                pair_copy(i, o).wait_recv()
                far_out[i, o - 1] = (acc[i] + pair_in[i, o].astype(F32)).astype(BF16)
                far_copy(i, o).start()

        def put_own(cols, value):
            acc[i, :, cols] = value

        project(i, hd, put_own)

    @pl.when(pos >= 2)
    def _():
        med_copy(0).wait_recv()

        @pl.when(pos + 2 < n_seq)
        def _():
            med_copy(1).start()

    for i in range(CHUNKS):
        edge(i)

    @pl.loop(0, n_seq)
    def _(o):
        @pl.when(o < pos)
        def _():
            remote(c_own, c_in.at[o], c_ss.at[o], c_rs.at[o], seq=o).wait_recv()

    @pl.loop(0, heads)
    def _(h):
        got = c_in[:, h].astype(F32)
        ck[h] = got[:, :n_coarse].reshape(n_seq * n_coarse, HEAD_DIM).astype(BF16)
        cvt[h] = got[:, n_coarse:].reshape(n_seq * n_coarse, HEAD_DIM).T.astype(BF16)

    loads[2].wait()

    @pl.when(pos >= 4)
    def _():
        med_copy(1).wait_recv()

    loads[3].wait()
    for i in range(CHUNKS):
        local(i)
        combine(i)
        mix(i)
    for i in range(CHUNKS):
        pair_copy(i, 0).wait_recv()
        total = acc[i] + pair_in[i, 0].astype(F32)
        for o in range(1, groups):
            far_copy(i, o).wait_recv()
            total = total + far_in[i, o - 1].astype(F32)
        out_ref[pl.ds(i * chunk, chunk), :] = total.astype(BF16)

    @pl.when(has_prev)
    def _():
        for i in range(CHUNKS):
            q_copy(i).wait_send()

    @pl.when(has_next)
    def _():
        for i in range(CHUNKS):
            le_copy(i).wait_send()

            @pl.loop(0, heads)
            def _(h):
                oe_copy(i, h).wait_send()

    @pl.when(pos + 2 < n_seq)
    def _():
        med_copy(0).wait_send()

    @pl.when((pos >= 2) & (pos + 2 < n_seq))
    def _():
        med_copy(1).wait_send()

    @pl.loop(0, n_seq)
    def _(to):
        @pl.when(to > pos)
        def _():
            c_copy(to).wait_send()

    for i in range(CHUNKS):
        for o in range(groups):
            pair_copy(i, o).wait_send()
            if o:
                far_copy(i, o).wait_send()


def body(n_seq, n_head, queries, keys, values, med_weight, coarse_weight, out_weight):
    tok, feat = queries.shape
    heads = feat // HEAD_DIM
    chunk = tok // CHUNKS
    width = out_weight.shape[1] // n_head
    groups = n_head // 2
    far = max(groups - 1, 1)
    n_med = tok // MED
    n_coarse = tok // COARSE
    wm = jnp.tile(med_weight, (1, 1, n_med)).reshape(2 * heads, 1, tok)
    wc = jnp.tile(coarse_weight, (1, 1, n_coarse)).reshape(2 * heads, 1, tok)
    dma = pltpu.SemaphoreType.DMA
    hbm = pl.BlockSpec(memory_space=pl.ANY)
    vmem = pl.BlockSpec(memory_space=pltpu.VMEM)
    V = pltpu.VMEM
    scratch = [
        V((tok, feat), BF16), V((tok, feat), BF16), V((tok, feat), BF16),
        V(out_weight.shape, BF16),
        V((heads, HEAD_DIM, tok), BF16),
        V((CHUNKS, chunk, feat), BF16),
        V((CHUNKS, heads, HEAD_DIM, chunk), BF16),
        V((CHUNKS, heads, 1, chunk), F32),
        V((CHUNKS, heads, HEAD_DIM, chunk), BF16),
        V((CHUNKS, heads, 1, chunk), F32),
        V((2, heads, n_med, HEAD_DIM), BF16),
        V((2, 2, heads, n_med, HEAD_DIM), BF16),
        V((heads, 2 * n_coarse, HEAD_DIM), BF16),
        V((n_seq, heads, 2 * n_coarse, HEAD_DIM), BF16),
        V((heads, n_seq * n_coarse, HEAD_DIM), BF16),
        V((heads, HEAD_DIM, n_seq * n_coarse), BF16),
        V((CHUNKS, heads, HEAD_DIM, chunk), F32),
        V((CHUNKS, heads, 1, chunk), F32),
        V((CHUNKS, heads, 1, chunk), F32),
        V((CHUNKS, chunk, feat), BF16),
        V((CHUNKS, groups, chunk, width), BF16),
        V((CHUNKS, groups, chunk, width), BF16),
        V((CHUNKS, far, chunk, width), BF16),
        V((CHUNKS, far, chunk, width), BF16),
        V((CHUNKS, chunk, width), F32),
        dma((4,)),
        dma((CHUNKS,)), dma((CHUNKS,)),
        dma((CHUNKS, heads)), dma((CHUNKS, heads)),
        dma((CHUNKS,)), dma((CHUNKS,)),
        dma((2,)), dma((2,)),
        dma((n_seq,)), dma((n_seq,)),
        dma((CHUNKS, groups)), dma((CHUNKS, groups)),
        dma((CHUNKS, far)), dma((CHUNKS, far)),
    ]
    return pl.pallas_call(
        functools.partial(kernel, n_seq, n_head),
        out_shape=jax.ShapeDtypeStruct((tok, width), BF16),
        in_specs=[hbm, hbm, hbm, vmem, vmem, hbm],
        out_specs=vmem,
        scratch_shapes=scratch,
        compiler_params=pltpu.CompilerParams(
            collective_id=0, has_side_effects=True, vmem_limit_bytes=60 * 1024 * 1024
        ),
    )(queries, keys, values, wm, wc, out_weight)


def solution(mesh):
    placed = (
        P("seq", "head"),
        P("seq", "head"),
        P("seq", "head"),
        P(None, "head", None),
        P(None, "head", None),
        P("head", None),
    )
    return jax.shard_map(
        functools.partial(body, mesh.shape["seq"], mesh.shape["head"]),
        mesh=mesh, in_specs=placed, out_specs=P("seq", "head"), check_vma=False,
    )
```

profile of v0, /device:TPU:8, one launch (start us, length us, event | category | flops | bytes accessed | tf_op | source)
XLA Modules:
  0.0 98.7 jit_solution(17421288573378883329)
XLA Ops:
  0.0 0.7 copy.8
  0.7 0.7 tile.18
  1.4 0.7 tile.19.wc_ref
  2.1 0.1 tile.16
  2.2 0.3 tile.17
  2.5 0.7 copy.9.wm_ref
  3.3 93.1 %shard_map.64 = bf16[512,1024]{1,0:T(8,128)(2,1)} custom-call(bf16[512,1024]{1,0:T(8,128)(2,1)} %q_hbm.1, bf16[512,1024]{1,0:T(8,128)(2,1)} %k_hbm.1, bf16[512,1024]{1,0:T(8,128)(2,1)} %v_hbm.1, f32[16,1,512]{2,1,0:T(1,128)} %copy.9.wm_ref, f32[16,1,512]{2,1,0:T(1,128)} %tile.19.wc_ref, bf16[1024,4096]{1,0:T(8,128)(2,1)} %w_hbm.1), custom_call_target="tpu_custom_call" | custom-call | tf_op jit(solution)/shard_map/pallas_call | solution.py:411
  96.4 2.3 %copy.11 = bf16[512,1024]{1,0:T(8,128)(2,1)} copy(bf16[512,1024]{1,0:T(8,128)(2,1)} %shard_map.64) | data formatting | bytes 2097152
where the time goes:
time: 98.9 us; the launch traced here: 98.7 us
  Pallas kernels  93.1 us (94%)
  local copies, waits for them, and re-layouts  5.51 us (6%)
    pallas_call x1, Pallas kernels, body(): pl.pallas_call(functools.partial(kernel, n_seq, n_head), out_shape=jax.Sh...  93.1 us
    unnamed x2, local copies, waits for them, and re-layouts  2.95 us

commit v1 on v0

v1 whole, which is shorter than its diff:
```python
import functools
import math

import jax
import jax.numpy as jnp
from jax import lax
from jax.experimental import pallas as pl
from jax.experimental.pallas import tpu as pltpu
from jax.sharding import PartitionSpec as P

MESH = pl.DeviceIdType.MESH
F32 = jnp.float32
BF16 = jnp.bfloat16
LOG2E = math.log2(math.e)


def mm(a, b):
    return jnp.dot(a, b, preferred_element_type=F32)


def mm_nt(a, b):
    return lax.dot_general(a, b, (((1,), (1,)), ((), ())), preferred_element_type=F32)


def split(w):
    hi = w.astype(BF16)
    return hi, (w - hi.astype(F32)).astype(BF16)


def kernel(
    n_seq, n_head, q_hbm, k_hbm, v_hbm, wm_hbm, wc_hbm, w_hbm, out_hbm,
    q_v, k_v, v_v, wm_v, wc_v, pat, w_v, vt, q_in, oe_out, le_out, oe_in, le_in,
    med_own, med_in, c_own, c_in, ck, cvt, o_loc, m_loc, l_loc, attn, attn_in,
    far_out, far_in, acc, out_v,
    ld_sem, w_sem, wx_ss, wx_rs, q_ss, q_rs, oe_ss, oe_rs, le_ss, le_rs, med_ss, med_rs,
    c_ss, c_rs, at_ss, at_rs, far_ss, far_rs, out_sem,
):
    tok, feat = q_v.shape
    med, _, heads = wm_v.shape
    coarse = wc_v.shape[2]
    dim = feat // heads
    row = oe_in.shape[3]
    chunks = tok // row
    wide = 2 * row
    n_med = tok // med
    n_coarse = tok // coarse
    width = out_v.shape[1]
    tile = far_out.shape[4]
    tiles = width // tile
    scale = LOG2E / math.sqrt(dim)
    pos = lax.axis_index("seq")
    hd = lax.axis_index("head")
    groups = n_head // 2
    grp = hd // 2
    core = lax.rem(hd, 2)
    mate = grp * 2 + (1 - core)

    def remote(src, dst, ss, rs, **dev):
        return pltpu.make_async_remote_copy(
            src_ref=src, dst_ref=dst, send_sem=ss, recv_sem=rs,
            device_id=dev, device_id_type=MESH,
        )

    def hs(h):
        return pl.ds(pl.multiple_of(h * dim, dim), dim)

    loads = [
        pltpu.make_async_copy(s, d, ld_sem.at[n])
        for n, (s, d) in enumerate(
            ((wm_hbm, wm_v), (wc_hbm, wc_v), (k_hbm, k_v), (v_hbm, v_v), (q_hbm, q_v))
        )
    ]
    for ld in loads:
        ld.start()

    barrier = pltpu.get_barrier_semaphore()

    @pl.loop(1, n_seq)
    def _(d):
        pl.semaphore_signal(
            barrier, inc=1, device_id={"seq": lax.rem(pos + d, n_seq)}, device_id_type=MESH
        )

    @pl.loop(1, n_head)
    def _(d):
        pl.semaphore_signal(
            barrier, inc=1, device_id={"head": lax.rem(hd + d, n_head)}, device_id_type=MESH
        )

    @pl.loop(0, n_seq)
    def _(o):
        @pl.when(o >= pos)
        def _():
            c_in[o] = jnp.zeros(c_in.shape[1:], BF16)

    for slot in range(2):
        @pl.when(pos < 2 * slot + 2)
        def _():
            med_in[slot] = jnp.zeros(med_in.shape[1:], BF16)

    @pl.when(pos == 0)
    def _():
        oe_in[...] = jnp.zeros_like(oe_in)
        le_in[...] = jnp.full_like(le_in, -jnp.inf)

    loads[0].wait()
    loads[1].wait()
    for n, (src, size) in enumerate(((wm_v, med), (wc_v, coarse))):
        lane = lax.broadcasted_iota(jnp.int32, (size, row), 1)
        pick = lax.rem(lane, size) == lax.broadcasted_iota(jnp.int32, (size, row), 0)
        pick = jnp.where(pick, 1.0, 0.0).astype(BF16)
        for t in range(2):
            hi, lo = split(src[t] if n else src[:, t, :].T)
            pat[n, 0, t] = mm(hi, pick)
            pat[n, 1, t] = mm(lo, pick)

    pl.semaphore_wait(barrier, n_seq - 1 + n_head - 1)

    def rows(i):
        return pl.ds(i * row, row)

    def q_copy(i):
        return remote(
            q_hbm.at[rows(i)], q_in.at[rows(i)], q_ss.at[i], q_rs.at[i],
            seq=jnp.maximum(pos - 1, 0),
        )

    def oe_copy(i):
        return remote(
            oe_out.at[i], oe_in.at[i], oe_ss.at[i], oe_rs.at[i],
            seq=jnp.minimum(pos + 1, n_seq - 1),
        )

    def le_copy(i):
        return remote(
            le_out.at[i], le_in.at[i], le_ss.at[i], le_rs.at[i],
            seq=jnp.minimum(pos + 1, n_seq - 1),
        )

    def med_copy(slot):
        src = med_own if slot == 0 else med_in.at[0]
        return remote(
            src, med_in.at[slot], med_ss.at[slot], med_rs.at[slot],
            seq=jnp.minimum(pos + 2, n_seq - 1),
        )

    def c_copy(to):
        return remote(c_own, c_in.at[pos], c_ss.at[to], c_rs.at[pos], seq=to)

    def cols(g, side):
        return pl.ds(pl.multiple_of((g * 2 + side) * width, width), width)

    def w_load(g):
        return pltpu.make_async_copy(w_hbm.at[:, cols(g, core)], w_v.at[0, g], w_sem.at[g])

    def w_copy(g):
        return remote(
            w_hbm.at[:, cols(g, 1 - core)], w_v.at[1, g], wx_ss.at[g], wx_rs.at[g], head=mate
        )

    def at_copy(i):
        return remote(attn.at[rows(i)], attn_in.at[rows(i)], at_ss.at[i], at_rs.at[i], head=mate)

    def far_copy(i, o, j):
        return remote(
            far_out.at[i, o - 1, j], far_in.at[i, o - 1, j],
            far_ss.at[i, o - 1, j], far_rs.at[i, o - 1, j],
            head=lax.rem(grp + o, groups) * 2 + core,
        )

    def out_copy(i):
        return pltpu.make_async_copy(out_v.at[rows(i)], out_hbm.at[rows(i)], out_sem.at[i])

    has_prev = pos >= 1
    has_next = pos < n_seq - 1

    @pl.when(has_prev)
    def _():
        for i in range(chunks):
            q_copy(i).start()

    loads[2].wait()
    loads[3].wait()

    per = row // med
    sel = (lax.broadcasted_iota(jnp.int32, (per, row), 1) // med) == (
        lax.broadcasted_iota(jnp.int32, (per, row), 0)
    )
    c_row = lax.broadcasted_iota(jnp.int32, (2 * n_coarse, tok), 0)
    c_col = lax.broadcasted_iota(jnp.int32, (2 * n_coarse, tok), 1) // coarse

    @pl.loop(0, heads)
    def _(h):
        vt[h] = v_v[:, hs(h)].T
        pooled = []
        totals = []
        for t, src in enumerate((k_v, v_v)):
            one = pl.ds(h, 1)
            left = jnp.concatenate(
                [jnp.where(sel, pat[0, part, t, one, :], 0.0) for part in range(2)], axis=0
            ).astype(BF16)
            blocks = []
            for b in range(chunks):
                r = mm(left, src[rows(b), hs(h)])
                blocks.append((r[:per] + r[per:]).astype(BF16))
            pooled.append(jnp.concatenate(blocks, axis=0))
            hi, lo = (
                jnp.concatenate([pat[1, part, t, one, :]] * chunks, axis=1) for part in range(2)
            )
            left = jnp.where(c_col == c_row, hi, 0.0)
            left = jnp.where(c_col + n_coarse == c_row, lo, left).astype(BF16)
            r = mm(left, src[:, hs(h)])
            totals.append(r[:n_coarse] + r[n_coarse:])
        med_own[0, h] = pooled[0]
        med_own[1, h] = pooled[1].T
        c_own[h] = jnp.concatenate(totals, axis=0).astype(BF16)

    @pl.when(pos + 2 < n_seq)
    def _():
        med_copy(0).start()

    for g in range(groups):
        w_copy(g).start()
        w_load(g).start()

    @pl.loop(0, n_seq)
    def _(to):
        @pl.when(to > pos)
        def _():
            c_copy(to).start()

    loads[4].wait()

    def keep(i, h, o, m, total):
        for n in range(2):
            at = slice(n * row, (n + 1) * row)
            o_loc[2 * i + n, h] = o[:, at]
            m_loc[2 * i + n, pl.ds(h, 1), :] = m[:, at]
            l_loc[2 * i + n, pl.ds(h, 1), :] = total[:, at]

    def softmax_parts(parts, m, total, o):
        for s, vals in parts:
            p = jnp.exp2((s - m) * scale)
            total = total + jnp.sum(p, axis=0, keepdims=True)
            o = o + mm(vals, p.astype(BF16))
        return total, o

    def peak(parts):
        return functools.reduce(
            jnp.maximum, [jnp.max(s, axis=0, keepdims=True) for s, _ in parts]
        )

    def own(i):
        first = i * wide

        @pl.loop(0, heads)
        def _(h):
            q = q_v[pl.ds(first, wide), hs(h)]
            parts = []
            if first:
                s = mm_nt(k_v[pl.ds(0, first), hs(h)], q)
                parts.append((s, vt[h, :, pl.ds(0, first)]))
            s = mm_nt(k_v[pl.ds(first, wide), hs(h)], q)
            key_at = lax.broadcasted_iota(jnp.int32, (wide, wide), 0)
            query_at = lax.broadcasted_iota(jnp.int32, (wide, wide), 1)
            s = jnp.where(key_at <= query_at, s, -jnp.inf)
            parts.append((s, vt[h, :, pl.ds(first, wide)]))
            m = peak(parts)
            total, o = softmax_parts(parts, m, 0.0, 0.0)
            keep(i, h, o, m, total)

    def edge(i):
        @pl.when(has_next)
        def _():
            @pl.loop(0, heads)
            def _(h):
                q = q_in[pl.ds(i * wide, wide), hs(h)]
                s = mm_nt(k_v[:, hs(h)], q)
                s2 = jnp.where(pos >= 2, mm_nt(med_in[0, 0, h], q), -jnp.inf)
                parts = [(s, vt[h]), (s2, med_in[0, 1, h])]
                m = peak(parts)
                total, o = softmax_parts(parts, m, 0.0, 0.0)
                o = (o / total).astype(BF16)
                lse = m * scale + jnp.log2(total)
                for n in range(2):
                    at = slice(n * row, (n + 1) * row)
                    oe_out[2 * i + n, h] = o[:, at]
                    le_out[2 * i + n, pl.ds(h, 1), :] = lse[:, at]

    def await_queries(i):
        @pl.when(has_next)
        def _():
            q_copy(2 * i).wait_recv()
            q_copy(2 * i + 1).wait_recv()

    def send_edge(i):
        @pl.when(has_next)
        def _():
            for n in range(2):
                le_copy(2 * i + n).start()
                oe_copy(2 * i + n).start()

    def remote_parts(i):
        @pl.loop(0, heads)
        def _(h):
            q = q_v[pl.ds(i * wide, wide), hs(h)]
            parts = []
            for slot in range(2):
                s = mm_nt(med_in[slot, 0, h], q)
                parts.append((jnp.where(pos >= 2 * slot + 2, s, -jnp.inf), med_in[slot, 1, h]))
            s = mm_nt(ck[h], q)
            owner = lax.broadcasted_iota(jnp.int32, s.shape, 0) // n_coarse
            parts.append((jnp.where(owner < pos, s, -jnp.inf), cvt[h]))
            both = (2 * i, 2 * i + 1)
            old = jnp.concatenate([m_loc[c, pl.ds(h, 1), :] for c in both], axis=1)
            total = jnp.concatenate([l_loc[c, pl.ds(h, 1), :] for c in both], axis=1)
            o = jnp.concatenate([o_loc[c, h] for c in both], axis=1)
            m = jnp.maximum(old, peak(parts))
            a = jnp.exp2((old - m) * scale)
            total, o = softmax_parts(parts, m, total * a, o * a)
            keep(i, h, o, m, total)

    def combine(i):
        @pl.when(has_prev)
        def _():
            le_copy(i).wait_recv()
            oe_copy(i).wait_recv()

        mine = m_loc[i] * scale
        lse = le_in[i]
        top = jnp.maximum(mine, lse)
        a = jnp.exp2(mine - top)
        e = jnp.exp2(lse - top)
        inv = 1.0 / (l_loc[i] * a + e)
        a = a * inv
        e = e * inv
        for h in range(heads):
            o = o_loc[i, h] * a[h:h + 1] + oe_in[i, h].astype(F32) * e[h:h + 1]
            attn[rows(i), h * dim:(h + 1) * dim] = o.astype(BF16).T
        at_copy(i).start()

    def mix(i):
        waited = False
        for o in list(range(1, groups)) + [0]:
            g = lax.rem(grp + o, groups)

            for j in range(tiles):
                at = pl.ds(j * tile, tile)
                acc[i, :, at] = mm(attn[rows(i)], w_v[0, g, :, at])
            if not waited:
                at_copy(i).wait_recv()
                waited = True
            for j in range(tiles):
                at = pl.ds(j * tile, tile)
                value = acc[i, :, at] + mm(attn_in[rows(i)], w_v[1, g, :, at])
                if o:
                    far_out[i, o - 1, j] = value.astype(BF16)
                    far_copy(i, o, j).start()
                else:
                    acc[i, :, at] = value

    def final(i):
        for j in range(tiles):
            at = pl.ds(j * tile, tile)
            total = acc[i, :, at]
            for o in range(1, groups):
                far_copy(i, o, j).wait_recv()
                total = total + far_in[i, o - 1, j].astype(F32)
            out_v[rows(i), at] = total.astype(BF16)
        out_copy(i).start()

    for i in range(chunks // 2):
        own(i)

    @pl.when(pos >= 2)
    def _():
        med_copy(0).wait_recv()

        @pl.when(pos + 2 < n_seq)
        def _():
            med_copy(1).start()

    halves = chunks // 2
    await_queries(0)
    for i in range(halves):
        edge(i)
        if i + 1 < halves:
            await_queries(i + 1)
        if i + 2 >= halves:
            for n in range(i if i + 2 > halves else 0, i + 1):
                send_edge(n)

    @pl.loop(0, n_seq)
    def _(o):
        @pl.when(o < pos)
        def _():
            remote(c_own, c_in.at[o], c_ss.at[o], c_rs.at[o], seq=o).wait_recv()

    @pl.loop(0, heads)
    def _(h):
        got = c_in[:, h].astype(F32)
        ck[h] = got[:, :n_coarse].reshape(n_seq * n_coarse, dim).astype(BF16)
        cvt[h] = got[:, n_coarse:].reshape(n_seq * n_coarse, dim).T.astype(BF16)

    @pl.when(pos >= 4)
    def _():
        med_copy(1).wait_recv()

    for i in range(chunks // 2):
        remote_parts(i)

    for g in range(groups):
        w_load(g).wait()
        w_copy(g).wait_recv()

    for i in range(chunks):
        combine(i)
        mix(i)
        if i:
            final(i - 1)
    final(chunks - 1)

    @pl.when(has_prev)
    def _():
        for i in range(chunks):
            q_copy(i).wait_send()

    @pl.when(has_next)
    def _():
        for i in range(chunks):
            le_copy(i).wait_send()
            oe_copy(i).wait_send()

    @pl.when(pos + 2 < n_seq)
    def _():
        med_copy(0).wait_send()

    @pl.when((pos >= 2) & (pos + 2 < n_seq))
    def _():
        med_copy(1).wait_send()

    @pl.loop(0, n_seq)
    def _(to):
        @pl.when(to > pos)
        def _():
            c_copy(to).wait_send()

    for g in range(groups):
        w_copy(g).wait_send()
    for i in range(chunks):
        at_copy(i).wait_send()
        for o in range(1, groups):
            for j in range(tiles):
                far_copy(i, o, j).wait_send()
    for i in range(chunks):
        out_copy(i).wait()


def body(n_seq, n_head, queries, keys, values, med_weight, coarse_weight, out_weight):
    tok, feat = queries.shape
    heads, med = med_weight.shape[1:]
    dim = feat // heads
    row = dim
    chunks = tok // row
    width = out_weight.shape[1] // n_head
    groups = n_head // 2
    far = max(groups - 1, 1)
    tile = math.gcd(width, 4 * dim)
    tiles = width // tile
    n_med = tok // med
    n_coarse = tok // coarse_weight.shape[2]
    dma = pltpu.SemaphoreType.DMA
    hbm = pl.BlockSpec(memory_space=pl.ANY)
    V = pltpu.VMEM
    scratch = [
        V((tok, feat), BF16), V((tok, feat), BF16), V((tok, feat), BF16),
        V((med, 2, heads), F32), V(coarse_weight.shape, F32),
        V((2, 2, 2, heads, row), F32),
        V((2, groups, feat, width), BF16),
        V((heads, dim, tok), BF16),
        V((tok, feat), BF16),
        V((chunks, heads, dim, row), BF16),
        V((chunks, heads, row), F32),
        V((chunks, heads, dim, row), BF16),
        V((chunks, heads, row), F32),
        V((2, heads, n_med, dim), BF16),
        V((2, 2, heads, n_med, dim), BF16),
        V((heads, 2 * n_coarse, dim), BF16),
        V((n_seq, heads, 2 * n_coarse, dim), BF16),
        V((heads, n_seq * n_coarse, dim), BF16),
        V((heads, dim, n_seq * n_coarse), BF16),
        V((chunks, heads, dim, row), F32),
        V((chunks, heads, row), F32),
        V((chunks, heads, row), F32),
        V((tok, feat), BF16),
        V((tok, feat), BF16),
        V((chunks, far, tiles, row, tile), BF16),
        V((chunks, far, tiles, row, tile), BF16),
        V((chunks, row, width), F32),
        V((tok, width), BF16),
        dma((5,)), dma((groups,)), dma((groups,)), dma((groups,)),
        dma((chunks,)), dma((chunks,)),
        dma((chunks,)), dma((chunks,)),
        dma((chunks,)), dma((chunks,)),
        dma((2,)), dma((2,)),
        dma((n_seq,)), dma((n_seq,)),
        dma((chunks,)), dma((chunks,)),
        dma((chunks, far, tiles)), dma((chunks, far, tiles)),
        dma((chunks,)),
    ]
    return pl.pallas_call(
        functools.partial(kernel, n_seq, n_head),
        out_shape=jax.ShapeDtypeStruct((tok, width), BF16),
        in_specs=[hbm] * 6,
        out_specs=hbm,
        scratch_shapes=scratch,
        compiler_params=pltpu.CompilerParams(
            collective_id=0, has_side_effects=True, vmem_limit_bytes=60 * 1024 * 1024
        ),
    )(queries, keys, values, med_weight.transpose(2, 0, 1), coarse_weight, out_weight)


def solution(mesh):
    placed = (
        P("seq", "head"),
        P("seq", "head"),
        P("seq", "head"),
        P(None, "head", None),
        P(None, "head", None),
        P("head", None),
    )
    return jax.shard_map(
        functools.partial(body, mesh.shape["seq"], mesh.shape["head"]),
        mesh=mesh, in_specs=placed, out_specs=P("seq", "head"), check_vma=False,
    )
```

time: 98.9 us -> 75.1 us (0.76)
  the two profiles are of different devices: /device:TPU:8 before, /device:TPU:25 now
where the time goes in v1:
time: 75.1 us; the launch traced here: 73.7 us
  Pallas kernels  70.1 us (93%)
  local copies, waits for them, and re-layouts  3.54 us (5%)
    pallas_call x1, Pallas kernels, body(): pl.pallas_call(functools.partial(kernel, n_seq, n_head), out_shape=jax.Sh...  70.1 us
    unnamed x2, local copies, waits for them, and re-layouts  3.54 us

profile of v1, /device:TPU:25, one launch (start us, length us, event | category | flops | bytes accessed | tf_op | source)
XLA Modules:
  0.0 73.7 jit_solution(2202920232008907179)
XLA Ops:
  0.0 1.3 %copy.9 = f32[2,8,4]{1,0,2:T(2,128)} copy(f32[2,8,4]{1,2,0:T(4,128)} %param.9) | data formatting | bytes 512 | tf_op args[3]
  1.3 70.1 %shard_map.64 = bf16[512,1024]{1,0:T(8,128)(2,1)} custom-call(bf16[512,1024]{1,0:T(8,128)(2,1)} %q_hbm.1, bf16[512,1024]{1,0:T(8,128)(2,1)} %k_hbm.1, bf16[512,1024]{1,0:T(8,128)(2,1)} %v_hbm.1, f32[4,2,8]{2,1,0:T(2,128)} %bitcast.3, f32[2,8,64]{2,1,0:T(8,128)} %wc_hbm.1, bf16[1024,4096]{1,0:T(8,128)(2,1)} %w_hbm.1), custom_call_target="tpu_custom_call" | custom-call | tf_op jit(solution)/shard_map/pallas_call | solution.py:511
  71.4 2.3 %copy.11 = bf16[512,1024]{1,0:T(8,128)(2,1)} copy(bf16[512,1024]{1,0:T(8,128)(2,1)} %shard_map.64) | data formatting | bytes 2097152

commit v2 on v1

v2 whole, which is shorter than its diff:
```python
import functools
import math

import jax
import jax.numpy as jnp
from jax import lax
from jax.experimental import pallas as pl
from jax.experimental.pallas import tpu as pltpu
from jax.sharding import PartitionSpec as P

MESH = pl.DeviceIdType.MESH
F32 = jnp.float32
BF16 = jnp.bfloat16
LOG2E = math.log2(math.e)


def mm(a, b):
    return jnp.dot(a, b, preferred_element_type=F32)


def mm_nt(a, b):
    return lax.dot_general(a, b, (((1,), (1,)), ((), ())), preferred_element_type=F32)


def split(w):
    hi = w.astype(BF16)
    return hi, (w - hi.astype(F32)).astype(BF16)


def row_pieces(tok, row):
    cuts = list(range(0, tok, row)) + [tok - row // 2, tok]
    return list(zip(cuts[:-1], cuts[1:]))


def kernel(
    n_seq, n_head, q_hbm, k_hbm, v_hbm, wm_hbm, wc_hbm, w_hbm, out_ref,
    q_v, k_v, v_v, wm_v, wc_v, pat, w_v, vt, q_in, oe_out, le_out, oe_in, le_in,
    med_own, med_in, c_own, c_in, ck, cvt, o_loc, m_loc, l_loc, a_loc, e_col, o_rows,
    attn, attn_in, far_out, far_in, acc,
    ld_sem, w_sem, wx_ss, wx_rs, q_ss, q_rs, oe_ss, oe_rs, le_ss, le_rs, med_ss, med_rs,
    c_ss, c_rs, at_ss, at_rs, far_ss, far_rs,
):
    tok, feat = q_v.shape
    _, med, heads = wm_v.shape
    coarse = wc_v.shape[2]
    dim = feat // heads
    row = dim
    chunks = tok // row
    wide = 2 * row
    halves = tok // wide
    pieces = row_pieces(tok, row)
    n_med = tok // med
    n_coarse = tok // coarse
    width = out_ref.shape[1]
    tile = far_out.shape[3]
    tiles = width // tile
    scale = LOG2E / math.sqrt(dim)
    pos = lax.axis_index("seq")
    hd = lax.axis_index("head")
    groups = n_head // 2
    grp = hd // 2
    core = lax.rem(hd, 2)
    mate = grp * 2 + (1 - core)

    def remote(src, dst, ss, rs, **dev):
        return pltpu.make_async_remote_copy(
            src_ref=src, dst_ref=dst, send_sem=ss, recv_sem=rs,
            device_id=dev, device_id_type=MESH,
        )

    def hs(h):
        return pl.ds(pl.multiple_of(h * dim, dim), dim)

    loads = [
        pltpu.make_async_copy(s, d, ld_sem.at[n])
        for n, (s, d) in enumerate(
            ((wm_hbm, wm_v), (wc_hbm, wc_v), (k_hbm, k_v), (v_hbm, v_v), (q_hbm, q_v))
        )
    ]
    for ld in loads:
        ld.start()

    barrier = pltpu.get_barrier_semaphore()

    @pl.loop(1, n_seq)
    def _(d):
        pl.semaphore_signal(
            barrier, inc=1, device_id={"seq": lax.rem(pos + d, n_seq)}, device_id_type=MESH
        )

    @pl.loop(1, n_head)
    def _(d):
        pl.semaphore_signal(
            barrier, inc=1, device_id={"head": lax.rem(hd + d, n_head)}, device_id_type=MESH
        )

    @pl.loop(0, n_seq)
    def _(o):
        @pl.when(o >= pos)
        def _():
            c_in[o] = jnp.zeros(c_in.shape[1:], BF16)

    for slot in range(2):
        @pl.when(pos < 2 * slot + 2)
        def _():
            med_in[slot] = jnp.zeros(med_in.shape[1:], BF16)

    @pl.when(pos == 0)
    def _():
        oe_in[...] = jnp.zeros_like(oe_in)
        le_in[...] = jnp.full_like(le_in, -jnp.inf)

    loads[0].wait()
    loads[1].wait()
    for n, (src, size) in enumerate(((wm_v, med), (wc_v, coarse))):
        lane = lax.broadcasted_iota(jnp.int32, (size, row), 1)
        pick = lax.rem(lane, size) == lax.broadcasted_iota(jnp.int32, (size, row), 0)
        pick = jnp.where(pick, 1.0, 0.0).astype(BF16)
        for t in range(2):
            hi, lo = split(src[t] if n else src[t].T)
            pat[n, 0, t] = mm(hi, pick)
            pat[n, 1, t] = mm(lo, pick)

    pl.semaphore_wait(barrier, n_seq - 1 + n_head - 1)

    def rows(i):
        return pl.ds(i * row, row)

    def q_copy(i):
        return remote(
            q_hbm.at[rows(i)], q_in.at[rows(i)], q_ss.at[i], q_rs.at[i],
            seq=jnp.maximum(pos - 1, 0),
        )

    def part(c):
        return pl.ds(pieces[c][0], pieces[c][1] - pieces[c][0])

    def oe_copy(c):
        return remote(
            oe_out.at[part(c)], oe_in.at[part(c)], oe_ss.at[c], oe_rs.at[c],
            seq=jnp.minimum(pos + 1, n_seq - 1),
        )

    def le_copy(i):
        return remote(
            le_out.at[i], le_in.at[i], le_ss.at[i], le_rs.at[i],
            seq=jnp.minimum(pos + 1, n_seq - 1),
        )

    def med_copy(slot, t):
        src = med_own if slot == 0 else med_in.at[0]
        return remote(
            src.at[t], med_in.at[slot, t], med_ss.at[slot, t], med_rs.at[slot, t],
            seq=jnp.minimum(pos + 2, n_seq - 1),
        )

    def c_copy(to):
        return remote(c_own, c_in.at[pos], c_ss.at[to], c_rs.at[pos], seq=to)

    def cols(g, side):
        return pl.ds(pl.multiple_of((g * 2 + side) * width, width), width)

    def w_load(g):
        return pltpu.make_async_copy(w_hbm.at[:, cols(g, core)], w_v.at[0, g], w_sem.at[g])

    def w_copy(g):
        return remote(
            w_hbm.at[:, cols(g, 1 - core)], w_v.at[1, g], wx_ss.at[g], wx_rs.at[g], head=mate
        )

    def at_copy(c):
        return remote(attn.at[part(c)], attn_in.at[part(c)], at_ss.at[c], at_rs.at[c], head=mate)

    def far_copy(c, o, j):
        return remote(
            far_out.at[o - 1, j, part(c)], far_in.at[o - 1, j, part(c)],
            far_ss.at[c, o - 1, j], far_rs.at[c, o - 1, j],
            head=lax.rem(grp + o, groups) * 2 + core,
        )

    has_prev = pos >= 1
    has_next = pos < n_seq - 1

    @pl.when(has_prev)
    def _():
        for i in range(chunks):
            q_copy(i).start()

    for g in range(groups):
        w_copy(g).start()
        w_load(g).start()
    loads[2].wait()
    loads[3].wait()

    per = row // med
    sel = (lax.broadcasted_iota(jnp.int32, (per, row), 1) // med) == (
        lax.broadcasted_iota(jnp.int32, (per, row), 0)
    )
    c_row = lax.broadcasted_iota(jnp.int32, (2 * n_coarse, tok), 0)
    c_col = lax.broadcasted_iota(jnp.int32, (2 * n_coarse, tok), 1) // coarse

    for t, src in enumerate((k_v, v_v)):
        @pl.loop(0, heads)
        def _(h):
            one = pl.ds(h, 1)
            left = jnp.concatenate(
                [jnp.where(sel, pat[0, n, t, one, :], 0.0) for n in range(2)], axis=0
            ).astype(BF16)
            blocks = []
            for b in range(chunks):
                r = mm(left, src[rows(b), hs(h)])
                blocks.append((r[:per] + r[per:]).astype(BF16))
            pooled = jnp.concatenate(blocks, axis=0)
            med_own[t, h] = pooled.T if t else pooled

        @pl.when(pos + 2 < n_seq)
        def _():
            med_copy(0, t).start()

    @pl.loop(0, heads)
    def _(h):
        vt[h] = v_v[:, hs(h)].T
        totals = []
        for t, src in enumerate((k_v, v_v)):
            hi, lo = (
                jnp.concatenate([pat[1, n, t, pl.ds(h, 1), :]] * chunks, axis=1)
                for n in range(2)
            )
            left = jnp.where(c_col == c_row, hi, 0.0)
            left = jnp.where(c_col + n_coarse == c_row, lo, left).astype(BF16)
            r = mm(left, src[:, hs(h)])
            totals.append(r[:n_coarse] + r[n_coarse:])
        c_own[h] = jnp.concatenate(totals, axis=0).astype(BF16)

    @pl.loop(0, n_seq)
    def _(to):
        @pl.when(to > pos)
        def _():
            c_copy(to).start()

    loads[4].wait()

    def keep(i, h, o, m, total):
        o_loc[i, h] = o
        m_loc[i, pl.ds(h, 1), :] = m
        l_loc[i, pl.ds(h, 1), :] = total

    def softmax_parts(parts, m, total, o):
        for s, vals in parts:
            p = jnp.exp2((s - m) * scale)
            total = total + jnp.sum(p, axis=0, keepdims=True)
            o = o + mm(vals, p.astype(BF16))
        return total, o

    def peak(parts):
        return functools.reduce(
            jnp.maximum, [jnp.max(s, axis=0, keepdims=True) for s, _ in parts]
        )

    def own(i):
        first = i * wide

        @pl.loop(0, heads, unroll=2)
        def _(h):
            q = q_v[pl.ds(first, wide), hs(h)]
            parts = []
            if first:
                s = mm_nt(k_v[pl.ds(0, first), hs(h)], q)
                parts.append((s, vt[h, :, pl.ds(0, first)]))
            s = mm_nt(k_v[pl.ds(first, wide), hs(h)], q)
            key_at = lax.broadcasted_iota(jnp.int32, (wide, wide), 0)
            query_at = lax.broadcasted_iota(jnp.int32, (wide, wide), 1)
            s = jnp.where(key_at <= query_at, s, -jnp.inf)
            parts.append((s, vt[h, :, pl.ds(first, wide)]))
            m = peak(parts)
            total, o = softmax_parts(parts, m, 0.0, 0.0)
            keep(i, h, o, m, total)

    def edge(i):
        @pl.when(has_next)
        def _():
            @pl.loop(0, heads, unroll=2)
            def _(h):
                q = q_in[pl.ds(i * wide, wide), hs(h)]
                s = mm_nt(k_v[:, hs(h)], q)
                s2 = jnp.where(pos >= 2, mm_nt(med_in[0, 0, h], q), -jnp.inf)
                parts = [(s, vt[h]), (s2, med_in[0, 1, h])]
                m = peak(parts)
                total, o = softmax_parts(parts, m, 0.0, 0.0)
                oe_out[pl.ds(i * wide, wide), hs(h)] = (o / total).astype(BF16).T
                le_out[i, pl.ds(h, 1), :] = m * scale + jnp.log2(total)

            le_copy(i).start()

    def await_queries(i):
        @pl.when(has_next)
        def _():
            q_copy(2 * i).wait_recv()
            q_copy(2 * i + 1).wait_recv()

    def send_edge(i):
        @pl.when(has_next)
        def _():
            for c, (first, _) in enumerate(pieces):
                if first // wide == i:
                    oe_copy(c).start()

    def remote_parts(i):
        @pl.loop(0, heads, unroll=2)
        def _(h):
            q = q_v[pl.ds(i * wide, wide), hs(h)]
            parts = []
            for slot in range(2):
                s = mm_nt(med_in[slot, 0, h], q)
                parts.append((jnp.where(pos >= 2 * slot + 2, s, -jnp.inf), med_in[slot, 1, h]))
            s = mm_nt(ck[h], q)
            owner = lax.broadcasted_iota(jnp.int32, s.shape, 0) // n_coarse
            parts.append((jnp.where(owner < pos, s, -jnp.inf), cvt[h]))
            old = m_loc[i, pl.ds(h, 1), :]
            total = l_loc[i, pl.ds(h, 1), :]
            o = o_loc[i, h]
            m = jnp.maximum(old, peak(parts))
            a = jnp.exp2((old - m) * scale)
            total, o = softmax_parts(parts, m, total * a, o * a)
            keep(i, h, o, m, total)

    def prepare(i):
        @pl.when(has_prev)
        def _():
            le_copy(i).wait_recv()

        mine = m_loc[i] * scale
        lse = le_in[i]
        top = jnp.maximum(mine, lse)
        a = jnp.exp2(mine - top)
        e = jnp.exp2(lse - top)
        inv = 1.0 / (l_loc[i] * a + e)
        a_loc[...] = a * inv
        e_col[pl.ds(i * wide, wide), :] = (e * inv).T

        @pl.loop(0, heads)
        def _(h):
            o_rows[pl.ds(i * wide, wide), hs(h)] = (o_loc[i, h] * a_loc[pl.ds(h, 1), :]).T

    def combine(c):
        @pl.when(has_prev)
        def _():
            oe_copy(c).wait_recv()

        for h in range(heads):
            at = slice(h * dim, (h + 1) * dim)
            o = o_rows[part(c), at] + oe_in[part(c), at].astype(F32) * e_col[part(c), h:h + 1]
            attn[part(c), at] = o.astype(BF16)
        at_copy(c).start()

    def mix(c):
        waited = False
        for o in list(range(1, groups)) + [0]:
            g = lax.rem(grp + o, groups)
            for j in range(tiles):
                at = pl.ds(j * tile, tile)
                acc[part(c), at] = mm(attn[part(c)], w_v[0, g, :, at])
            if not waited:
                at_copy(c).wait_recv()
                waited = True
            for j in range(tiles):
                at = pl.ds(j * tile, tile)
                value = acc[part(c), at] + mm(attn_in[part(c)], w_v[1, g, :, at])
                if o:
                    far_out[o - 1, j, part(c)] = value.astype(BF16)
                    far_copy(c, o, j).start()
                else:
                    acc[part(c), at] = value

    def final(c):
        for j in range(tiles):
            at = pl.ds(j * tile, tile)
            total = acc[part(c), at]
            for o in range(1, groups):
                far_copy(c, o, j).wait_recv()
                total = total + far_in[o - 1, j, part(c)].astype(F32)
            out_ref[part(c), at] = total.astype(BF16)

    def pass_on(t):
        @pl.when(pos >= 2)
        def _():
            med_copy(0, t).wait_recv()

            @pl.when(pos + 2 < n_seq)
            def _():
                med_copy(1, t).start()

    for i in range(halves):
        own(i)
        if i < 2:
            pass_on(i)

    await_queries(0)
    for i in range(halves):
        edge(i)
        if i + 1 < halves:
            await_queries(i + 1)
        send_edge(i)

    @pl.loop(0, n_seq)
    def _(o):
        @pl.when(o < pos)
        def _():
            remote(c_own, c_in.at[o], c_ss.at[o], c_rs.at[o], seq=o).wait_recv()

    @pl.loop(0, heads)
    def _(h):
        got = c_in[:, h].astype(F32)
        ck[h] = got[:, :n_coarse].reshape(n_seq * n_coarse, dim).astype(BF16)
        cvt[h] = got[:, n_coarse:].reshape(n_seq * n_coarse, dim).T.astype(BF16)

    @pl.when(pos >= 4)
    def _():
        med_copy(1, 0).wait_recv()
        med_copy(1, 1).wait_recv()

    for g in range(groups):
        w_load(g).wait()
        w_copy(g).wait_recv()

    for c, (first, _) in enumerate(pieces):
        if first % wide == 0:
            @pl.when(has_prev)
            def _():
                remote_parts(first // wide)

            prepare(first // wide)
        combine(c)
        mix(c)
    for c in range(len(pieces)):
        final(c)

    @pl.when(has_prev)
    def _():
        for i in range(chunks):
            q_copy(i).wait_send()

    @pl.when(has_next)
    def _():
        for i in range(halves):
            le_copy(i).wait_send()
        for c in range(len(pieces)):
            oe_copy(c).wait_send()

    @pl.when(pos + 2 < n_seq)
    def _():
        med_copy(0, 0).wait_send()
        med_copy(0, 1).wait_send()

    @pl.when((pos >= 2) & (pos + 2 < n_seq))
    def _():
        med_copy(1, 0).wait_send()
        med_copy(1, 1).wait_send()

    @pl.loop(0, n_seq)
    def _(to):
        @pl.when(to > pos)
        def _():
            c_copy(to).wait_send()

    for g in range(groups):
        w_copy(g).wait_send()
    for c in range(len(pieces)):
        at_copy(c).wait_send()
        for o in range(1, groups):
            for j in range(tiles):
                far_copy(c, o, j).wait_send()


def body(n_seq, n_head, queries, keys, values, med_weight, coarse_weight, out_weight):
    tok, feat = queries.shape
    heads, med = med_weight.shape[1:]
    dim = feat // heads
    row = dim
    chunks = tok // row
    wide = 2 * row
    halves = tok // wide
    pieces = len(row_pieces(tok, row))
    width = out_weight.shape[1] // n_head
    groups = n_head // 2
    far = max(groups - 1, 1)
    tile = math.gcd(width, 4 * dim)
    tiles = width // tile
    n_med = tok // med
    n_coarse = tok // coarse_weight.shape[2]
    dma = pltpu.SemaphoreType.DMA
    hbm = pl.BlockSpec(memory_space=pl.ANY)
    V = pltpu.VMEM
    scratch = [
        V((tok, feat), BF16), V((tok, feat), BF16), V((tok, feat), BF16),
        V((2, med, heads), F32), V(coarse_weight.shape, F32),
        V((2, 2, 2, heads, row), F32),
        V((2, groups, feat, width), BF16),
        V((heads, dim, tok), BF16),
        V((tok, feat), BF16),
        V((tok, feat), BF16),
        V((halves, heads, wide), F32),
        V((tok, feat), BF16),
        V((halves, heads, wide), F32),
        V((2, heads, n_med, dim), BF16),
        V((2, 2, heads, n_med, dim), BF16),
        V((heads, 2 * n_coarse, dim), BF16),
        V((n_seq, heads, 2 * n_coarse, dim), BF16),
        V((heads, n_seq * n_coarse, dim), BF16),
        V((heads, dim, n_seq * n_coarse), BF16),
        V((halves, heads, dim, wide), F32),
        V((halves, heads, wide), F32),
        V((halves, heads, wide), F32),
        V((heads, wide), F32),
        V((tok, heads), F32),
        V((tok, feat), F32),
        V((tok, feat), BF16),
        V((tok, feat), BF16),
        V((far, tiles, tok, tile), BF16),
        V((far, tiles, tok, tile), BF16),
        V((tok, width), F32),
        dma((5,)), dma((groups,)), dma((groups,)), dma((groups,)),
        dma((chunks,)), dma((chunks,)),
        dma((pieces,)), dma((pieces,)),
        dma((halves,)), dma((halves,)),
        dma((2, 2)), dma((2, 2)),
        dma((n_seq,)), dma((n_seq,)),
        dma((pieces,)), dma((pieces,)),
        dma((pieces, far, tiles)), dma((pieces, far, tiles)),
    ]
    return pl.pallas_call(
        functools.partial(kernel, n_seq, n_head),
        out_shape=jax.ShapeDtypeStruct((tok, width), BF16),
        in_specs=[hbm] * 6,
        out_specs=pl.BlockSpec(memory_space=pltpu.VMEM),
        scratch_shapes=scratch,
        compiler_params=pltpu.CompilerParams(
            collective_id=0, has_side_effects=True, vmem_limit_bytes=48 * 1024 * 1024
        ),
    )(*(
        pltpu.with_memory_space_constraint(x, pltpu.HBM)
        for x in (
            queries, keys, values, med_weight.transpose(0, 2, 1), coarse_weight, out_weight
        )
    ))


def solution(mesh):
    placed = (
        P("seq", "head"),
        P("seq", "head"),
        P("seq", "head"),
        P(None, "head", None),
        P(None, "head", None),
        P("head", None),
    )
    return jax.shard_map(
        functools.partial(body, mesh.shape["seq"], mesh.shape["head"]),
        mesh=mesh, in_specs=placed, out_specs=P("seq", "head"), check_vma=False,
    )
```

time: 75.1 us -> 69.9 us (0.931)
  the two profiles are of different devices: /device:TPU:25 before, /device:TPU:16 now
where the time goes in v2:
time: 69.9 us; the launch traced here: 69.7 us
  Pallas kernels  68.7 us (98%)
  local copies, waits for them, and re-layouts  0.97 us (1%)
    pallas_call x1, Pallas kernels, body(): pl.pallas_call(functools.partial(kernel, n_seq, n_head), out_shape=jax.Sh...  68.7 us

profile of v2, /device:TPU:16, one launch (start us, length us, event | category | flops | bytes accessed | tf_op | source)
XLA Modules:
  0.0 69.7 jit_solution(17978074673063221062)
XLA Ops:
  0.0 68.7 %shard_map.64 = bf16[512,1024]{1,0:T(8,128)(2,1)S(1)} custom-call(bf16[512,1024]{1,0:T(8,128)(2,1)} %q_hbm.1, bf16[512,1024]{1,0:T(8,128)(2,1)} %k_hbm.1, bf16[512,1024]{1,0:T(8,128)(2,1)} %v_hbm.1, f32[2,4,8]{2,1,0:T(4,128)} %bitcast.1, f32[2,8,64]{2,1,0:T(8,128)} %wc_hbm.1, bf16[1024,4096]{1,0:T(8,128)(2,1)} %w_hbm.1), custom_call_target="tpu_custom_call" | custom-call | tf_op jit(solution)/shard_map/pallas_call | solution.py:531
  68.7 1.0 %copy.8 = bf16[512,1024]{1,0:T(8,128)(2,1)} copy(bf16[512,1024]{1,0:T(8,128)(2,1)S(1)} %shard_map.64) | data formatting | bytes 2097152

commit v3 on v2

--- a/solution.py
+++ b/solution.py
@@ -35,7 +35,7 @@
 def kernel(
     n_seq, n_head, q_hbm, k_hbm, v_hbm, wm_hbm, wc_hbm, w_hbm, out_ref,
     q_v, k_v, v_v, wm_v, wc_v, pat, w_v, vt, q_in, oe_out, le_out, oe_in, le_in,
-    med_own, med_in, c_own, c_in, ck, cvt, o_loc, m_loc, l_loc, a_loc, e_col, o_rows,
+    med_own, med_in, c_in, ck, cvt, o_loc, m_loc, l_loc, a_loc, e_col, o_rows,
     attn, attn_in, far_out, far_in, acc,
     ld_sem, w_sem, wx_ss, wx_rs, q_ss, q_rs, oe_ss, oe_rs, le_ss, le_rs, med_ss, med_rs,
     c_ss, c_rs, at_ss, at_rs, far_ss, far_rs,
@@ -77,16 +77,20 @@
             ((wm_hbm, wm_v), (wc_hbm, wc_v), (k_hbm, k_v), (v_hbm, v_v), (q_hbm, q_v))
         )
     ]
-    for ld in loads:
+    for ld in loads[:4]:
         ld.start()
 
     barrier = pltpu.get_barrier_semaphore()
 
-    @pl.loop(1, n_seq)
-    def _(d):
-        pl.semaphore_signal(
-            barrier, inc=1, device_id={"seq": lax.rem(pos + d, n_seq)}, device_id_type=MESH
-        )
+    near_by = [(d, pos + d) for d in (-2, -1, 1, 2)]
+    others = n_head - 1
+    for d, to in near_by:
+        there = to >= 0 if d < 0 else to < n_seq
+        others = others + jnp.where(there, 1, 0)
+
+        @pl.when(there)
+        def _():
+            pl.semaphore_signal(barrier, inc=1, device_id={"seq": to}, device_id_type=MESH)
 
     @pl.loop(1, n_head)
     def _(d):
@@ -96,7 +100,7 @@
 
     @pl.loop(0, n_seq)
     def _(o):
-        @pl.when(o >= pos)
+        @pl.when(o > pos)
         def _():
             c_in[o] = jnp.zeros(c_in.shape[1:], BF16)
 
@@ -121,10 +125,34 @@
             pat[n, 0, t] = mm(hi, pick)
             pat[n, 1, t] = mm(lo, pick)
 
-    pl.semaphore_wait(barrier, n_seq - 1 + n_head - 1)
-
     def rows(i):
         return pl.ds(i * row, row)
+
+    per = row // med
+    sel = (lax.broadcasted_iota(jnp.int32, (per, row), 1) // med) == (
+        lax.broadcasted_iota(jnp.int32, (per, row), 0)
+    )
+    loads[2].wait()
+    loads[3].wait()
+
+    @pl.when(pos + 2 < n_seq)
+    def _():
+        for t, src in enumerate((k_v, v_v)):
+            @pl.loop(0, heads, unroll=2)
+            def _(h):
+                one = pl.ds(h, 1)
+                left = jnp.concatenate(
+                    [jnp.where(sel, pat[0, n, t, one, :], 0.0) for n in range(2)], axis=0
+                ).astype(BF16)
+                blocks = []
+                for b in range(chunks):
+                    r = mm(left, src[rows(b), hs(h)])
+                    blocks.append((r[:per] + r[per:]).astype(BF16))
+                pooled = jnp.concatenate(blocks, axis=0)
+                med_own[t, h] = pooled.T if t else pooled
+
+    pl.semaphore_wait(barrier, others)
+    loads[4].start()
 
     def q_copy(i):
         return remote(
@@ -154,8 +182,17 @@
             seq=jnp.minimum(pos + 2, n_seq - 1),
         )
 
-    def c_copy(to):
-        return remote(c_own, c_in.at[pos], c_ss.at[to], c_rs.at[pos], seq=to)
+    def c_copy(o, step):
+        return remote(
+            c_in.at[o], c_in.at[o], c_ss.at[step - 1, o], c_rs.at[o],
+            seq=jnp.minimum(pos + step, n_seq - 1),
+        )
+
+    def c_send(o, act):
+        for step in (2, 1):
+            @pl.when(pos + step < n_seq)
+            def _():
+                act(c_copy(o, step))
 
     def cols(g, side):
         return pl.ds(pl.multiple_of((g * 2 + side) * width, width), width)
@@ -186,36 +223,15 @@
         for i in range(chunks):
             q_copy(i).start()
 
+    @pl.when(pos + 2 < n_seq)
+    def _():
+        med_copy(0, 0).start()
+
     for g in range(groups):
         w_copy(g).start()
         w_load(g).start()
-    loads[2].wait()
-    loads[3].wait()
-
-    per = row // med
-    sel = (lax.broadcasted_iota(jnp.int32, (per, row), 1) // med) == (
-        lax.broadcasted_iota(jnp.int32, (per, row), 0)
-    )
     c_row = lax.broadcasted_iota(jnp.int32, (2 * n_coarse, tok), 0)
     c_col = lax.broadcasted_iota(jnp.int32, (2 * n_coarse, tok), 1) // coarse
-
-    for t, src in enumerate((k_v, v_v)):
-        @pl.loop(0, heads)
-        def _(h):
-            one = pl.ds(h, 1)
-            left = jnp.concatenate(
-                [jnp.where(sel, pat[0, n, t, one, :], 0.0) for n in range(2)], axis=0
-            ).astype(BF16)
-            blocks = []
-            for b in range(chunks):
-                r = mm(left, src[rows(b), hs(h)])
-                blocks.append((r[:per] + r[per:]).astype(BF16))
-            pooled = jnp.concatenate(blocks, axis=0)
-            med_own[t, h] = pooled.T if t else pooled
-
-        @pl.when(pos + 2 < n_seq)
-        def _():
-            med_copy(0, t).start()
 
     @pl.loop(0, heads)
     def _(h):
@@ -230,13 +246,13 @@
             left = jnp.where(c_col + n_coarse == c_row, lo, left).astype(BF16)
             r = mm(left, src[:, hs(h)])
             totals.append(r[:n_coarse] + r[n_coarse:])
-        c_own[h] = jnp.concatenate(totals, axis=0).astype(BF16)
-
-    @pl.loop(0, n_seq)
-    def _(to):
-        @pl.when(to > pos)
-        def _():
-            c_copy(to).start()
+        c_in[pos, h] = jnp.concatenate(totals, axis=0).astype(BF16)
+
+    c_send(pos, lambda copy: copy.start())
+
+    @pl.when(pos + 2 < n_seq)
+    def _():
+        med_copy(0, 1).start()
 
     loads[4].wait()
 
@@ -298,31 +314,58 @@
             q_copy(2 * i).wait_recv()
             q_copy(2 * i + 1).wait_recv()
 
-    def send_edge(i):
+    def send_edge(low, high):
         @pl.when(has_next)
         def _():
             for c, (first, _) in enumerate(pieces):
-                if first // wide == i:
+                if low <= first < high:
                     oe_copy(c).start()
 
-    def remote_parts(i):
+    def merge(i, h, parts):
+        old = m_loc[i, pl.ds(h, 1), :]
+        m = jnp.maximum(old, peak(parts))
+        a = jnp.exp2((old - m) * scale)
+        total, o = softmax_parts(parts, m, l_loc[i, pl.ds(h, 1), :] * a, o_loc[i, h] * a)
+        keep(i, h, o, m, total)
+
+    def near(i):
         @pl.loop(0, heads, unroll=2)
         def _(h):
             q = q_v[pl.ds(i * wide, wide), hs(h)]
-            parts = []
-            for slot in range(2):
-                s = mm_nt(med_in[slot, 0, h], q)
-                parts.append((jnp.where(pos >= 2 * slot + 2, s, -jnp.inf), med_in[slot, 1, h]))
+            merge(i, h, [(mm_nt(med_in[0, 0, h], q), med_in[0, 1, h])])
+
+    def far_keys():
+        @pl.loop(0, n_seq)
+        def _(o):
+            @pl.when((o < pos) & (lax.rem(pos - o + n_seq * 2, 2) == 1))
+            def _():
+                c_copy(o, 1).wait_recv()
+
+        @pl.loop(0, heads)
+        def _(h):
+            got = c_in[:, h].astype(F32)
+            ck[h] = got[:, :n_coarse].reshape(n_seq * n_coarse, dim).astype(BF16)
+            cvt[h] = got[:, n_coarse:].reshape(n_seq * n_coarse, dim).T.astype(BF16)
+
+        @pl.when(pos >= 4)
+        def _():
+            med_copy(1, 0).wait_recv()
+            med_copy(1, 1).wait_recv()
+
+        @pl.when(has_prev)
+        def _():
+            distant(0)
+
+    def distant(i):
+        @pl.loop(0, heads, unroll=2)
+        def _(h):
+            q = q_v[pl.ds(i * wide, wide), hs(h)]
+            s = mm_nt(med_in[1, 0, h], q)
+            parts = [(jnp.where(pos >= 4, s, -jnp.inf), med_in[1, 1, h])]
             s = mm_nt(ck[h], q)
             owner = lax.broadcasted_iota(jnp.int32, s.shape, 0) // n_coarse
             parts.append((jnp.where(owner < pos, s, -jnp.inf), cvt[h]))
-            old = m_loc[i, pl.ds(h, 1), :]
-            total = l_loc[i, pl.ds(h, 1), :]
-            o = o_loc[i, h]
-            m = jnp.maximum(old, peak(parts))
-            a = jnp.exp2((old - m) * scale)
-            total, o = softmax_parts(parts, m, total * a, o * a)
-            keep(i, h, o, m, total)
+            merge(i, h, parts)
 
     def prepare(i):
         @pl.when(has_prev)
@@ -392,42 +435,58 @@
 
     for i in range(halves):
         own(i)
-        if i < 2:
-            pass_on(i)
-
+
+    def relay(here):
+        @pl.when(here)
+        def _():
+            @pl.loop(0, n_seq)
+            def _(o):
+                @pl.when((o < pos) & (lax.rem(pos - o + n_seq * 2, 2) == 0))
+                def _():
+                    c_copy(o, 1).wait_recv()
+                    c_send(o, lambda copy: copy.start())
+
+    relay(pos < 4)
+    pass_on(0)
+    relay((pos >= 4) & (pos < 6))
+    pass_on(1)
     await_queries(0)
-    for i in range(halves):
+    edge(0)
+    odd = lax.rem(pos, 2) == 1
+    relay((pos >= 6) & jnp.logical_not(odd))
+
+    @pl.when(jnp.logical_not(odd))
+    def _():
+        send_edge(0, wide)
+
+    @pl.when(pos >= 2)
+    def _():
+        for i in range(halves):
+            near(i)
+
+
+    relay((pos >= 6) & odd)
+
+    for i in range(1, halves):
+        await_queries(i)
+        if i == 1:
+            @pl.when(odd)
+            def _():
+                send_edge(0, wide)
+
         edge(i)
-        if i + 1 < halves:
-            await_queries(i + 1)
-        send_edge(i)
-
-    @pl.loop(0, n_seq)
-    def _(o):
-        @pl.when(o < pos)
-        def _():
-            remote(c_own, c_in.at[o], c_ss.at[o], c_rs.at[o], seq=o).wait_recv()
-
-    @pl.loop(0, heads)
-    def _(h):
-        got = c_in[:, h].astype(F32)
-        ck[h] = got[:, :n_coarse].reshape(n_seq * n_coarse, dim).astype(BF16)
-        cvt[h] = got[:, n_coarse:].reshape(n_seq * n_coarse, dim).T.astype(BF16)
-
-    @pl.when(pos >= 4)
-    def _():
-        med_copy(1, 0).wait_recv()
-        med_copy(1, 1).wait_recv()
-
+        send_edge(i * wide, (i + 1) * wide)
+    far_keys()
     for g in range(groups):
         w_load(g).wait()
         w_copy(g).wait_recv()
 
     for c, (first, _) in enumerate(pieces):
         if first % wide == 0:
-            @pl.when(has_prev)
-            def _():
-                remote_parts(first // wide)
+            if first:
+                @pl.when(has_prev)
+                def _():
+                    distant(first // wide)
 
             prepare(first // wide)
         combine(c)
@@ -458,10 +517,10 @@
         med_copy(1, 1).wait_send()
 
     @pl.loop(0, n_seq)
-    def _(to):
-        @pl.when(to > pos)
-        def _():
-            c_copy(to).wait_send()
+    def _(o):
+        @pl.when((o <= pos) & (lax.rem(pos - o + n_seq * 2, 2) == 0))
+        def _():
+            c_send(o, lambda copy: copy.wait_send())
 
     for g in range(groups):
         w_copy(g).wait_send()
@@ -504,7 +563,6 @@
         V((halves, heads, wide), F32),
         V((2, heads, n_med, dim), BF16),
         V((2, 2, heads, n_med, dim), BF16),
-        V((heads, 2 * n_coarse, dim), BF16),
         V((n_seq, heads, 2 * n_coarse, dim), BF16),
         V((heads, n_seq * n_coarse, dim), BF16),
         V((heads, dim, n_seq * n_coarse), BF16),
@@ -524,7 +582,7 @@
         dma((pieces,)), dma((pieces,)),
         dma((halves,)), dma((halves,)),
         dma((2, 2)), dma((2, 2)),
-        dma((n_seq,)), dma((n_seq,)),
+        dma((2, n_seq)), dma((n_seq,)),
         dma((pieces,)), dma((pieces,)),
         dma((pieces, far, tiles)), dma((pieces, far, tiles)),
     ]

time: 69.9 us -> 68.1 us (0.974)
  the two profiles are of different devices: /device:TPU:16 before, /device:TPU:25 now
where the time goes in v3:
time: 68.1 us; the launch traced here: 67.6 us
  Pallas kernels  66.6 us (98%)
  local copies, waits for them, and re-layouts  0.97 us (1%)
    pallas_call x1, Pallas kernels, body(): pl.pallas_call(functools.partial(kernel, n_seq, n_head), out_shape=jax.Sh...  66.6 us

profile of v3, /device:TPU:25, one launch (start us, length us, event | category | flops | bytes accessed | tf_op | source)
XLA Modules:
  0.0 67.6 jit_solution(4879174963295247324)
XLA Ops:
  0.0 66.6 %shard_map.64 = bf16[512,1024]{1,0:T(8,128)(2,1)S(1)} custom-call(bf16[512,1024]{1,0:T(8,128)(2,1)} %q_hbm.1, bf16[512,1024]{1,0:T(8,128)(2,1)} %k_hbm.1, bf16[512,1024]{1,0:T(8,128)(2,1)} %v_hbm.1, f32[2,4,8]{2,1,0:T(4,128)} %bitcast.1, f32[2,8,64]{2,1,0:T(8,128)} %wc_hbm.1, bf16[1024,4096]{1,0:T(8,128)(2,1)} %w_hbm.1), custom_call_target="tpu_custom_call" | custom-call | tf_op jit(solution)/shard_map/pallas_call | solution.py:589
  66.6 1.0 %copy.8 = bf16[512,1024]{1,0:T(8,128)(2,1)} copy(bf16[512,1024]{1,0:T(8,128)(2,1)S(1)} %shard_map.64) | data formatting | bytes 2097152

commit v4 on v3

--- a/solution.py
+++ b/solution.py
@@ -295,7 +295,7 @@
     def edge(i):
         @pl.when(has_next)
         def _():
-            @pl.loop(0, heads, unroll=2)
+            @pl.loop(0, heads, unroll=4)
             def _(h):
                 q = q_in[pl.ds(i * wide, wide), hs(h)]
                 s = mm_nt(k_v[:, hs(h)], q)
@@ -329,7 +329,7 @@
         keep(i, h, o, m, total)
 
     def near(i):
-        @pl.loop(0, heads, unroll=2)
+        @pl.loop(0, heads, unroll=4)
         def _(h):
             q = q_v[pl.ds(i * wide, wide), hs(h)]
             merge(i, h, [(mm_nt(med_in[0, 0, h], q), med_in[0, 1, h])])
@@ -357,7 +357,7 @@
             distant(0)
 
     def distant(i):
-        @pl.loop(0, heads, unroll=2)
+        @pl.loop(0, heads, unroll=4)
         def _(h):
             q = q_v[pl.ds(i * wide, wide), hs(h)]
             s = mm_nt(med_in[1, 0, h], q)
@@ -397,23 +397,26 @@
         at_copy(c).start()
 
     def mix(c):
-        waited = False
-        for o in list(range(1, groups)) + [0]:
+        for o in range(1, groups):
             g = lax.rem(grp + o, groups)
             for j in range(tiles):
                 at = pl.ds(j * tile, tile)
                 acc[part(c), at] = mm(attn[part(c)], w_v[0, g, :, at])
-            if not waited:
+            if o == 1:
                 at_copy(c).wait_recv()
-                waited = True
             for j in range(tiles):
                 at = pl.ds(j * tile, tile)
                 value = acc[part(c), at] + mm(attn_in[part(c)], w_v[1, g, :, at])
-                if o:
-                    far_out[o - 1, j, part(c)] = value.astype(BF16)
-                    far_copy(c, o, j).start()
-                else:
-                    acc[part(c), at] = value
+                far_out[o - 1, j, part(c)] = value.astype(BF16)
+                far_copy(c, o, j).start()
+
+    def mix_own(i):
+        span = pl.ds(i * wide, wide)
+        for j in range(tiles):
+            at = pl.ds(j * tile, tile)
+            acc[span, at] = mm(attn[span], w_v[0, grp, :, at]) + mm(
+                attn_in[span], w_v[1, grp, :, at]
+            )
 
     def final(c):
         for j in range(tiles):
@@ -468,15 +471,21 @@
     relay((pos >= 6) & odd)
 
     for i in range(1, halves):
-        await_queries(i)
+        @pl.when(odd)
+        def _():
+            await_queries(i)
+            if i == 1:
+                send_edge(0, wide)
+
         if i == 1:
-            @pl.when(odd)
-            def _():
-                send_edge(0, wide)
+            far_keys()
+
+        @pl.when(jnp.logical_not(odd))
+        def _():
+            await_queries(i)
 
         edge(i)
         send_edge(i * wide, (i + 1) * wide)
-    far_keys()
     for g in range(groups):
         w_load(g).wait()
         w_copy(g).wait_recv()
@@ -491,6 +500,11 @@
             prepare(first // wide)
         combine(c)
         mix(c)
+    if groups == 1:
+        for c in range(len(pieces)):
+            at_copy(c).wait_recv()
+    for i in range(halves):
+        mix_own(i)
     for c in range(len(pieces)):
         final(c)
 

time: 68.1 us -> 67.7 us (level)
  no operation moved by 1% of the time
where the time goes in v4:
time: 67.7 us; the launch traced here: 67.5 us
  Pallas kernels  66.5 us (98%)
  local copies, waits for them, and re-layouts  0.97 us (1%)
    pallas_call x1, Pallas kernels, body(): pl.pallas_call(functools.partial(kernel, n_seq, n_head), out_shape=jax.Sh...  66.5 us

profile of v4, /device:TPU:25, one launch (start us, length us, event | category | flops | bytes accessed | tf_op | source)
XLA Modules:
  0.0 67.5 jit_solution(10883120804211032559)
XLA Ops:
  0.0 66.5 %shard_map.64 = bf16[512,1024]{1,0:T(8,128)(2,1)S(1)} custom-call(bf16[512,1024]{1,0:T(8,128)(2,1)} %q_hbm.1, bf16[512,1024]{1,0:T(8,128)(2,1)} %k_hbm.1, bf16[512,1024]{1,0:T(8,128)(2,1)} %v_hbm.1, f32[2,4,8]{2,1,0:T(4,128)} %bitcast.1, f32[2,8,64]{2,1,0:T(8,128)} %wc_hbm.1, bf16[1024,4096]{1,0:T(8,128)(2,1)} %w_hbm.1), custom_call_target="tpu_custom_call" | custom-call | tf_op jit(solution)/shard_map/pallas_call | solution.py:603
  66.5 1.0 %copy.8 = bf16[512,1024]{1,0:T(8,128)(2,1)} copy(bf16[512,1024]{1,0:T(8,128)(2,1)S(1)} %shard_map.64) | data formatting | bytes 2097152
